TPU v7x, 32 devices: a whole 2x2x4 slice. The times are simulated.
32 devices in a mesh: src: 4 (over y, x), blk: 8 (over z, core).
Axes of the slice: x: 2, y: 2, z: 4, core: 2. Of those that a mesh axis runs over, the one named last changes fastest.
Arguments:
- values: float32 [4, 512, 32, 128], P('src', 'blk'), may hold values from -0.25 to 0.25
- diagonal: float32 [4, 512, 128], P('src', 'blk'), may hold values from 0.55 to 0.95
- rhs_parts: float32 [4, 512, 128], P('src', 'blk'), may hold values from -24 to 24
- owner_map: int32 [512, 128], P('blk'), may hold values from 0 to 3
- columns: int32 [512, 32, 128], P('blk'), may hold values from 0 to 1073741823
- destination: int32 [512, 1], P('blk'), may hold values from 0 to 7; in each aligned block of 64 rows (0 to 63, 64 to 127, ...) at most 16 rows name the same one
- order_keys: int32 [512], P('blk'), may hold values from 0 to 511, each once
Outputs:
- solution: float32 [512, 128], P('blk')
Inputs may be any that keep to these rules, and one draw needn't show every extreme that they name: `destination`: among the row blocks of one index of blk no owner is named more than 16 times, some owner is named exactly 16 times, and every owner is named by some block. `order_keys`: each key appears once.
All inputs are finite; a program needn't handle non-finite values.
Results may differ from a plain program's by a relative error of at most 0.0003.
Values sent between devices are 32-bit elements; how exact they have to be, the bound alone decides.
No kernel may reach another device: no remote copies, remote signals or barrier semaphores. Data moves between devices by JAX's collectives and lax.ppermute only.
A program may use at most 64 MiB of HBM per device.

v0:
```python
import jax
import jax.numpy as jnp
from jax import lax
from jax.sharding import PartitionSpec as P

SWEEPS = 3


def tile_matrix(block_vals, block_cols, tile_rows):
    slot_count = block_vals.shape[0]
    stored = block_vals.shape[1]
    groups = 8
    lanes = jnp.remainder(block_cols, 2 * tile_rows)
    targets = jnp.arange(2 * tile_rows, dtype=jnp.int32)
    grouped_vals = block_vals.reshape(groups, slot_count // groups, stored, tile_rows)
    grouped_lanes = lanes.reshape(groups, slot_count // groups, stored, tile_rows)

    def build(pair):
        group_vals, group_lanes = pair
        picked = jnp.where(group_lanes[..., None] == targets, group_vals[..., None], 0.0)
        return jnp.sum(picked, axis=1)

    dense = lax.map(build, (grouped_vals, grouped_lanes))
    return dense.reshape(slot_count, tile_rows, 2 * tile_rows)


def on_device(values, diagonal, rhs_parts, owner_map, columns, destination, order_keys):
    owners = lax.axis_size("blk")
    part_count = lax.axis_size("src")
    tile_count = destination.shape[0]
    stored = values.shape[2]
    tile_rows = values.shape[3]
    per_peer = 2 * tile_count // owners
    slot_count = owners * per_peer
    owner_of = destination[:, 0]
    tile_ids = jnp.arange(tile_count, dtype=jnp.int32)
    slot_ids = jnp.arange(slot_count, dtype=jnp.int32)
    earlier = (owner_of[None, :] == owner_of[:, None]) & (tile_ids[None, :] < tile_ids[:, None])
    position = jnp.sum(earlier, axis=1)
    slot_of = owner_of * per_peer + position
    slot_hits = slot_of[None, :] == slot_ids[:, None]
    filled = jnp.any(slot_hits, axis=1)
    source_tile = jnp.sum(jnp.where(slot_hits, tile_ids[None, :], 0), axis=1)
    is_owned = owner_map == lax.axis_index("src")
    own_rhs = jnp.where(is_owned, rhs_parts[0], 0.0)
    send_vals = jnp.where(filled[:, None, None], values[0][source_tile], 0.0)
    send_diag = jnp.where(filled[:, None], diagonal[0][source_tile], 0.0)
    send_rhs = jnp.where(filled[:, None], own_rhs[source_tile], 0.0)
    send_cols = columns[source_tile]
    send_keys = jnp.where(filled, order_keys[source_tile], -1)
    quarter = stored // part_count
    part_vals = lax.psum_scatter(send_vals, "src", scatter_dimension=1, tiled=True)
    sum_diag, sum_rhs = lax.psum((send_diag, send_rhs), "src")
    part_cols = lax.dynamic_slice_in_dim(send_cols, lax.axis_index("src") * quarter, quarter, 1)
    got_vals, got_diag, got_rhs = (
        lax.all_to_all(part_vals, "blk", split_axis=0, concat_axis=0, tiled=True),
        lax.all_to_all(sum_diag, "blk", split_axis=0, concat_axis=0, tiled=True),
        lax.all_to_all(sum_rhs, "blk", split_axis=0, concat_axis=0, tiled=True),
    )
    got_cols, got_keys = (
        lax.all_to_all(part_cols, "blk", split_axis=0, concat_axis=0, tiled=True),
        lax.all_to_all(send_keys, "blk", split_axis=0, concat_axis=0, tiled=True),
    )
    is_live = got_keys >= 0
    tile_total = jnp.sum(is_live)
    smaller = is_live[None, :] & (got_keys[None, :] < got_keys[:, None])
    tile_rank = jnp.sum(smaller, axis=1)
    rank_hits = is_live[None, :] & (tile_rank[None, :] == slot_ids[:, None])
    holder = jnp.sum(jnp.where(rank_hits, slot_ids[None, :], 0), axis=1)
    occupied = slot_ids < tile_total
    block_vals = jnp.where(occupied[:, None, None], got_vals[holder], 0.0)
    block_cols = got_cols[holder]
    right_side = jnp.where(occupied[:, None], got_rhs[holder], 0.0)
    block_diag = jnp.where(occupied[:, None], got_diag[holder], 1.0)
    dense = tile_matrix(block_vals, block_cols, tile_rows)
    following = jnp.remainder(slot_ids + 1, tile_total)
    iterate = jnp.zeros((slot_count, tile_rows), jnp.float32)
    for sweep_index in range(SWEEPS):
        nearby = jnp.concatenate([iterate, iterate[following]], axis=1)
        partial_sum = jnp.sum(dense * nearby[:, None, :], axis=2)
        summed = lax.psum(partial_sum, "src")
        iterate = jnp.where(occupied[:, None], (right_side - summed) / block_diag, 0.0)
    in_slots = jnp.where(is_live[:, None], iterate[tile_rank], 0.0)
    returned = lax.all_to_all(in_slots, "blk", split_axis=0, concat_axis=0, tiled=True)
    return returned[slot_of]


def solution(mesh):
    placed = (
        P("src", "blk", None, None),
        P("src", "blk", None),
        P("src", "blk", None),
        P("blk", None),
        P("blk", None, None),
        P("blk", None),
        P("blk"),
    )
    return jax.shard_map(
        on_device, mesh=mesh, in_specs=placed, out_specs=P("blk", None), check_vma=False
    )
```

profile of v0, /device:TPU:0, one launch (start us, length us, event | category | flops | bytes accessed | tf_op | source)
XLA Modules:
  0.0 320.4 jit_solution(3956767261336183481)
XLA Ops:
  6.6 0.9 convert_reduce_fusion.1
  7.5 0.7 multiply_add_fusion
  8.4 0.8 gather_fusion.5
  9.2 1.6 broadcast_select_fusion
  10.8 1.6 gather_fusion
  12.4 0.7 select_n.147
  13.1 6.4 %all-to-all-start = ((s32[8,16,1]{1,2,0:T(1,128)}), s32[8,16,1]{1,2,0:T(1,128)S(1)}, u32[]{:S(2)}, u32[]{:S(2)}) async-start(s32[8,16,1]{1,2,0:T(1,128)} %bitcast.3), calls=%async_computation | async-start | bytes 8192 | tf_op jit(solution)/shard_map/all_to_all | solution.py:62
  19.4 2.2 gather_fusion.3
  21.6 0.9 constant_dynamic-slice_fusion
  22.5 2.4 all-to-all-done
  24.9 3.5 %all-to-all-start.2 = ((s32[128,8,128]{2,1,0:T(8,128)}), s32[128,8,128]{2,1,0:T(8,128)S(1)}, u32[]{:S(2)}, u32[]{:S(2)}) async-start(s32[128,8,128]{2,1,0:T(8,128)} %constant_dynamic-slice_fusion), calls=%async_computation.2 | async-start | bytes 1048576 | tf_op jit(solution)/shard_map/all_to_all | solution.py:61
  28.5 0.6 gather_fusion.1
  29.1 0.6 gather_fusion.8
  29.8 0.7 broadcast_select_fusion.4
  30.5 0.5 broadcast.232
  31.0 0.7 reduce.7
  31.8 0.6 convert_reduce_fusion.2
  33.9 0.6 gather_fusion.7
  34.5 9.2 %all-to-all-done.2 = s32[128,8,128]{2,1,0:T(8,128)S(1)} async-done(((s32[128,8,128]{2,1,0:T(8,128)}), s32[128,8,128]{2,1,0:T(8,128)S(1)}, u32[]{:S(2)}, u32[]{:S(2)}) %all-to-all-start.2) | async-done | bytes 524320 | tf_op jit(solution)/shard_map/all_to_all | solution.py:61
  43.7 5.2 %reduce-scatter.2.cloned.1.call-done = f32[128,8,128]{2,1,0:T(8,128)} async-done(((f32[128,32,128]{2,1,0:T(8,128)}), f32[128,8,128]{2,1,0:T(8,128)}) %reduce-scatter.2.cloned.1.call-update) | async-done | bytes 524304 | tf_op jit(solution)/shard_map/reduce_scatter | solution.py:52
  48.9 4.6 %all-to-all-start.3 = ((f32[128,8,128]{2,1,0:T(8,128)}), f32[128,8,128]{2,1,0:T(8,128)S(1)}, u32[]{:S(2)}, u32[]{:S(2)}) async-start(f32[128,8,128]{2,1,0:T(8,128)} %reduce-scatter.2.cloned.1.call-done), calls=%async_computation.4 | async-start | bytes 1048576 | tf_op jit(solution)/shard_map/all_to_all | solution.py:56
  53.5 0.7 add_compare_fusion
  54.5 0.8 gather_fusion.4
  55.5 13.3 %all-to-all-done.3 = f32[128,8,128]{2,1,0:T(8,128)S(1)} async-done(((f32[128,8,128]{2,1,0:T(8,128)}), f32[128,8,128]{2,1,0:T(8,128)S(1)}, u32[]{:S(2)}, u32[]{:S(2)}) %all-to-all-start.3) | async-done | bytes 524320 | tf_op jit(solution)/shard_map/all_to_all | solution.py:56
  68.8 0.8 gather_fusion.6
  69.8 57.8 %while.11 = (s32[]{:T(128)}, f32[8,16,128,256]{3,2,1,0:T(8,128)}, s32[8,16,8,128]{3,2,1,0:T(8,128)S(1)}, f32[8,16,8,128]{3,2,1,0:T(8,128)S(1)}, s32[]{:T(128)}) while((s32[]{:T(128)}, f32[8,16,128,256]{3,2,1,0:T(8,128)}, s32[8,16,8,128]{3,2,1,0:T(8,128)S(1)}, f32[8,16,8,128]{3,2,1,0:T(8,128)S(1)}, s32[]{:T(128)}) %tuple.23), condition=%wide.region_10.11_spmd.clone, body=%wide.region_8.10_spmd.clone.sunk | while | flops 12058626 | bytes 6685253 | solution.py:23
  69.8 5.7 %select_reduce_fusion.4 = f32[16,128,256]{2,1,0:T(8,128)S(1)} fusion(f32[16,8,128]{2,1,0:T(8,128)S(1)} %dynamic-slice_bitcast_fusion.4, s32[16,8,128]{2,1,0:T(8,128)S(1)} %dynamic-slice_bitcast_fusion.5), kind=kLoop, calls=%fused_computation.16.clone.1 | loop fusion | flops 12058624 | bytes 2228224 | tf_op jit(solution)/shard_map/while/body/eval_jaxpr/reduce_sum | solution.py:21
  75.5 1.6 bitcast_dynamic-update-slice_fusion.2
  77.1 5.7 %select_reduce_fusion.4 = f32[16,128,256]{2,1,0:T(8,128)S(1)} fusion(f32[16,8,128]{2,1,0:T(8,128)S(1)} %dynamic-slice_bitcast_fusion.4, s32[16,8,128]{2,1,0:T(8,128)S(1)} %dynamic-slice_bitcast_fusion.5), kind=kLoop, calls=%fused_computation.16.clone.1 | loop fusion | flops 12058624 | bytes 2228224 | tf_op jit(solution)/shard_map/while/body/eval_jaxpr/reduce_sum | solution.py:21
  82.7 1.5 bitcast_dynamic-update-slice_fusion.2
  84.2 5.7 %select_reduce_fusion.4 = f32[16,128,256]{2,1,0:T(8,128)S(1)} fusion(f32[16,8,128]{2,1,0:T(8,128)S(1)} %dynamic-slice_bitcast_fusion.4, s32[16,8,128]{2,1,0:T(8,128)S(1)} %dynamic-slice_bitcast_fusion.5), kind=kLoop, calls=%fused_computation.16.clone.1 | loop fusion | flops 12058624 | bytes 2228224 | tf_op jit(solution)/shard_map/while/body/eval_jaxpr/reduce_sum | solution.py:21
  89.9 1.5 bitcast_dynamic-update-slice_fusion.2
  91.5 5.7 %select_reduce_fusion.4 = f32[16,128,256]{2,1,0:T(8,128)S(1)} fusion(f32[16,8,128]{2,1,0:T(8,128)S(1)} %dynamic-slice_bitcast_fusion.4, s32[16,8,128]{2,1,0:T(8,128)S(1)} %dynamic-slice_bitcast_fusion.5), kind=kLoop, calls=%fused_computation.16.clone.1 | loop fusion | flops 12058624 | bytes 2228224 | tf_op jit(solution)/shard_map/while/body/eval_jaxpr/reduce_sum | solution.py:21
  97.1 1.5 bitcast_dynamic-update-slice_fusion.2
  98.7 5.7 %select_reduce_fusion.4 = f32[16,128,256]{2,1,0:T(8,128)S(1)} fusion(f32[16,8,128]{2,1,0:T(8,128)S(1)} %dynamic-slice_bitcast_fusion.4, s32[16,8,128]{2,1,0:T(8,128)S(1)} %dynamic-slice_bitcast_fusion.5), kind=kLoop, calls=%fused_computation.16.clone.1 | loop fusion | flops 12058624 | bytes 2228224 | tf_op jit(solution)/shard_map/while/body/eval_jaxpr/reduce_sum | solution.py:21
  104.4 1.6 bitcast_dynamic-update-slice_fusion.2
  106.0 5.7 %select_reduce_fusion.4 = f32[16,128,256]{2,1,0:T(8,128)S(1)} fusion(f32[16,8,128]{2,1,0:T(8,128)S(1)} %dynamic-slice_bitcast_fusion.4, s32[16,8,128]{2,1,0:T(8,128)S(1)} %dynamic-slice_bitcast_fusion.5), kind=kLoop, calls=%fused_computation.16.clone.1 | loop fusion | flops 12058624 | bytes 2228224 | tf_op jit(solution)/shard_map/while/body/eval_jaxpr/reduce_sum | solution.py:21
  111.6 1.5 bitcast_dynamic-update-slice_fusion.2
  113.1 5.7 %select_reduce_fusion.4 = f32[16,128,256]{2,1,0:T(8,128)S(1)} fusion(f32[16,8,128]{2,1,0:T(8,128)S(1)} %dynamic-slice_bitcast_fusion.4, s32[16,8,128]{2,1,0:T(8,128)S(1)} %dynamic-slice_bitcast_fusion.5), kind=kLoop, calls=%fused_computation.16.clone.1 | loop fusion | flops 12058624 | bytes 2228224 | tf_op jit(solution)/shard_map/while/body/eval_jaxpr/reduce_sum | solution.py:21
  118.8 1.6 bitcast_dynamic-update-slice_fusion.2
  120.4 5.7 %select_reduce_fusion.4 = f32[16,128,256]{2,1,0:T(8,128)S(1)} fusion(f32[16,8,128]{2,1,0:T(8,128)S(1)} %dynamic-slice_bitcast_fusion.4, s32[16,8,128]{2,1,0:T(8,128)S(1)} %dynamic-slice_bitcast_fusion.5), kind=kLoop, calls=%fused_computation.16.clone.1 | loop fusion | flops 12058624 | bytes 2228224 | tf_op jit(solution)/shard_map/while/body/eval_jaxpr/reduce_sum | solution.py:21
  126.1 1.5 bitcast_dynamic-update-slice_fusion.2
  127.6 8.6 %multiply_reduce_fusion.2 = f32[8,16,128]{2,1,0:T(8,128)} fusion(f32[8,16,128,256]{3,2,1,0:T(8,128)} %get-tuple-element.32, f32[8,16,256]{2,1,0:T(8,128)S(1)} %bitcast.63), kind=kLoop, calls=%fused_computation.22 | loop fusion | flops 8372224 | bytes 16973824 | tf_op jit(solution)/shard_map/reduce_sum | solution.py:80
  136.2 41.3 %all-reduce.10.cloned.1.call-done = (f32[128,128]{1,0:T(8,128)}, f32[8,16,128]{2,1,0:T(8,128)}, f32[8,16,128]{2,1,0:T(8,128)}) async-done(((f32[128,128]{1,0:T(8,128)}, f32[8,16,128]{2,1,0:T(8,128)}, f32[8,16,128]{2,1,0:T(8,128)}), (f32[128,128]{1,0:T(8,128)}, f32[8,16,128]{2,1,0:T(8,128)}, f32[8,16,128]{2,1,0:T(8,128)})) %all-reduce.10.cloned.1.call-update) | async-done | bytes 196624 | tf_op jit(solution)/shard_map/psum | solution.py:81
  177.5 10.5 %all_to_all.52 = f32[8,16,128]{2,1,0:T(8,128)S(1)} all-to-all(f32[8,16,128]{2,1,0:T(8,128)} %get-tuple-element.53), channel_id=1, replica_groups=mesh['src'=4,'blk'=8] {'blk'}, dimensions={0} | all-to-all | bytes 131072 | tf_op jit(solution)/shard_map/all_to_all | solution.py:58
  188.0 3.3 %all-to-all-start.4 = ((f32[8,16,128]{2,1,0:T(8,128)}), f32[8,16,128]{2,1,0:T(8,128)S(1)}, u32[]{:S(2)}, u32[]{:S(2)}) async-start(f32[8,16,128]{2,1,0:T(8,128)} %get-tuple-element.52), calls=%async_computation.5 | async-start | bytes 131072 | tf_op jit(solution)/shard_map/all_to_all | solution.py:57
  191.4 0.7 iota_compare_fusion.4
  192.1 0.6 gather_fusion.2
  192.7 4.5 %all-to-all-done.4 = f32[8,16,128]{2,1,0:T(8,128)S(1)} async-done(((f32[8,16,128]{2,1,0:T(8,128)}), f32[8,16,128]{2,1,0:T(8,128)S(1)}, u32[]{:S(2)}, u32[]{:S(2)}) %all-to-all-start.4) | async-done | bytes 65568 | tf_op jit(solution)/shard_map/all_to_all | solution.py:57
  197.2 0.6 gather_fusion.9
  197.9 0.9 divide_select_fusion.2
  198.8 0.6 gather_fusion.10
  199.5 8.6 %multiply_reduce_fusion.1 = f32[8,16,128]{2,1,0:T(8,128)} fusion(f32[8,16,128,256]{3,2,1,0:T(8,128)} %get-tuple-element.32, f32[8,16,256]{2,1,0:T(8,128)S(1)} %bitcast.65), kind=kLoop, calls=%fused_computation.21 | loop fusion | flops 8372224 | bytes 16973824 | tf_op jit(solution)/shard_map/reduce_sum | solution.py:80
  208.4 39.3 %all-reduce.6.cloned.1.call-done = f32[128,128]{1,0:T(8,128)} async-done(((f32[128,128]{1,0:T(8,128)}), f32[128,128]{1,0:T(8,128)}) %all-reduce.6.cloned.1.call-update) | async-done | bytes 65552 | tf_op jit(solution)/shard_map/psum | solution.py:81
  247.6 0.9 divide_select_fusion.1
  248.6 0.6 gather_fusion.11
  249.2 8.6 %multiply_reduce_fusion = f32[8,16,128]{2,1,0:T(8,128)} fusion(f32[8,16,128,256]{3,2,1,0:T(8,128)} %get-tuple-element.32, f32[8,16,256]{2,1,0:T(8,128)S(1)} %bitcast.64), kind=kLoop, calls=%fused_computation.20 | loop fusion | flops 8372224 | bytes 16973824 | tf_op jit(solution)/shard_map/reduce_sum | solution.py:80
  257.9 42.0 %all-reduce.8.cloned.1.call-done = f32[128,128]{1,0:T(8,128)} async-done(((f32[128,128]{1,0:T(8,128)}), f32[128,128]{1,0:T(8,128)}) %all-reduce.8.cloned.1.call-update) | async-done | bytes 65552 | tf_op jit(solution)/shard_map/psum | solution.py:81
  299.9 0.9 divide_select_fusion
  300.8 0.6 gather_fusion.12
  301.4 0.7 broadcast_select_fusion.2
  302.2 4.6 %all-to-all-start.5 = ((f32[8,16,128]{2,1,0:T(8,128)}), f32[8,16,128]{2,1,0:T(8,128)S(1)}, u32[]{:S(2)}, u32[]{:S(2)}) async-start(f32[8,16,128]{2,1,0:T(8,128)} %broadcast_select_fusion.2), calls=%async_computation.6 | async-start | bytes 131072 | tf_op jit(solution)/shard_map/all_to_all | solution.py:84
  306.8 5.9 %all-to-all-done.5 = f32[8,16,128]{2,1,0:T(8,128)S(1)} async-done(((f32[8,16,128]{2,1,0:T(8,128)}), f32[8,16,128]{2,1,0:T(8,128)S(1)}, u32[]{:S(2)}, u32[]{:S(2)}) %all-to-all-start.5) | async-done | bytes 65568 | tf_op jit(solution)/shard_map/all_to_all | solution.py:84
  312.7 1.2 gather_fusion.13
  (59 shorter events, 1.7 us)
Async XLA Ops:
  6.5 1.9 copy-start
  6.5 21.9 %copy-start.2 = (f32[1,64,128]{2,1,0:T(8,128)S(1)}, f32[1,64,128]{2,1,0:T(8,128)}, u32[]{:S(2)}) copy-start(f32[1,64,128]{2,1,0:T(8,128)} %param.11) | copy-start | bytes 98308
  6.5 21.9 %copy-start.3 = (s32[64,128]{1,0:T(8,128)S(1)}, s32[64,128]{1,0:T(8,128)}, u32[]{:S(2)}) copy-start(s32[64,128]{1,0:T(8,128)} %param.12) | copy-start | bytes 98308
  6.5 22.6 %copy-start.1 = (f32[1,64,128]{2,1,0:T(8,128)S(1)}, f32[1,64,128]{2,1,0:T(8,128)}, u32[]{:S(2)}) copy-start(f32[1,64,128]{2,1,0:T(8,128)} %param.10) | copy-start | bytes 98308
  6.5 42.3 %reduce-scatter.2.cloned.1.call-start = ((), (), s32[]{:S(2)}) async-start(), calls=%async_computation.7 | async-start | bytes 2621440 | tf_op jit(solution)/shard_map/reduce_scatter | solution.py:52
  13.1 11.9 %all-to-all-start = ((s32[8,16,1]{1,2,0:T(1,128)}), s32[8,16,1]{1,2,0:T(1,128)S(1)}, u32[]{:S(2)}, u32[]{:S(2)}) async-start(s32[8,16,1]{1,2,0:T(1,128)} %bitcast.3), calls=%async_computation | async-start | bytes 8192 | tf_op jit(solution)/shard_map/all_to_all | solution.py:62
  24.9 18.8 %all-to-all-start.2 = ((s32[128,8,128]{2,1,0:T(8,128)}), s32[128,8,128]{2,1,0:T(8,128)S(1)}, u32[]{:S(2)}, u32[]{:S(2)}) async-start(s32[128,8,128]{2,1,0:T(8,128)} %constant_dynamic-slice_fusion), calls=%async_computation.2 | async-start | bytes 1048576 | tf_op jit(solution)/shard_map/all_to_all | solution.py:61
  48.9 19.9 %all-to-all-start.3 = ((f32[128,8,128]{2,1,0:T(8,128)}), f32[128,8,128]{2,1,0:T(8,128)S(1)}, u32[]{:S(2)}, u32[]{:S(2)}) async-start(f32[128,8,128]{2,1,0:T(8,128)} %reduce-scatter.2.cloned.1.call-done), calls=%async_computation.4 | async-start | bytes 1048576 | tf_op jit(solution)/shard_map/all_to_all | solution.py:56
  53.5 124.0 %all-reduce.10.cloned.1.call-start = ((), (), s32[]{:S(2)}) async-start(), calls=%async_computation.10 | async-start | bytes 393216 | tf_op jit(solution)/shard_map/psum | solution.py:81
  188.0 9.2 %all-to-all-start.4 = ((f32[8,16,128]{2,1,0:T(8,128)}), f32[8,16,128]{2,1,0:T(8,128)S(1)}, u32[]{:S(2)}, u32[]{:S(2)}) async-start(f32[8,16,128]{2,1,0:T(8,128)} %get-tuple-element.52), calls=%async_computation.5 | async-start | bytes 131072 | tf_op jit(solution)/shard_map/all_to_all | solution.py:57
  191.4 56.3 %all-reduce.6.cloned.1.call-start = ((), (), s32[]{:S(2)}) async-start(), calls=%async_computation.8 | async-start | bytes 131072 | tf_op jit(solution)/shard_map/psum | solution.py:81
  199.5 107.3 %copy-start.4 = (s32[64,1]{0,1:T(1,128)S(1)}, s32[64,1]{0,1:T(1,128)}, u32[]{:S(2)}) copy-start(s32[64,1]{0,1:T(1,128)} %param.14) | copy-start | bytes 772
  208.1 91.7 %all-reduce.8.cloned.1.call-start = ((), (), s32[]{:S(2)}) async-start(), calls=%async_computation.9 | async-start | bytes 131072 | tf_op jit(solution)/shard_map/psum | solution.py:81
  302.2 10.5 %all-to-all-start.5 = ((f32[8,16,128]{2,1,0:T(8,128)}), f32[8,16,128]{2,1,0:T(8,128)S(1)}, u32[]{:S(2)}, u32[]{:S(2)}) async-start(f32[8,16,128]{2,1,0:T(8,128)} %broadcast_select_fusion.2), calls=%async_computation.6 | async-start | bytes 131072 | tf_op jit(solution)/shard_map/all_to_all | solution.py:84
Sparse Core Ops, SparseCore 0:
  10.9 37.9 reduce-scatter.1
  136.4 41.0 all-reduce.9
  208.2 39.3 all-reduce.5
  258.0 41.8 all-reduce.7
where the time goes:
time: 321 us; the launch traced here: 320 us
  waiting for transfers between devices  163 us (51%)
  other arithmetic  82.2 us (26%)
  local copies, waits for them, and re-layouts  27 us (8%)
  starting transfers between devices  22.7 us (7%)
  between operations  14.7 us (5%)
  blocking collectives  10.5 us (3%)
    psum x3, waiting for transfers between devices, on_device(): summed = lax.psum(partial_sum, 'src')  123 us
    reduce_sum x8, other arithmetic, build(): return jnp.sum(picked, axis=1)  45.3 us
    reduce_sum x3, other arithmetic, on_device(): partial_sum = jnp.sum(dense * nearby[:, None, :], axis=2)  25.9 us
    all_to_all x1, waiting for transfers between devices, on_device(): lax.all_to_all(part_vals, 'blk', split_axis=0, concat_axis=0, tiled=True)  13.3 us
    dynamic_update_slice x8, local copies, waits for them, and re-layouts, tile_matrix(): dense = lax.map(build, (grouped_vals, grouped_lanes))  12.3 us
    all_to_all x1, blocking collectives, on_device(): lax.all_to_all(sum_rhs, 'blk', split_axis=0, concat_axis=0, tiled=True)  10.5 us
    all_to_all x1, waiting for transfers between devices, on_device(): lax.all_to_all(part_cols, 'blk', split_axis=0, concat_axis=0, tiled=True)  9.16 us
  transfers between devices with their start and end apart: 9, of which 9 were waited for; matrix products, arithmetic and copies ran while one was open for 4% of the time, Pallas kernels for 0%

commit v1 on v0

--- a/solution.py
+++ b/solution.py
@@ -78,7 +78,9 @@
     for sweep_index in range(SWEEPS):
         nearby = jnp.concatenate([iterate, iterate[following]], axis=1)
         partial_sum = jnp.sum(dense * nearby[:, None, :], axis=2)
-        summed = lax.psum(partial_sum, "src")
+        summed = partial_sum
+        for hop in (1, 2):
+            summed = summed + lax.ppermute(summed, "src", [(dev, dev ^ hop) for dev in range(4)])
         iterate = jnp.where(occupied[:, None], (right_side - summed) / block_diag, 0.0)
     in_slots = jnp.where(is_live[:, None], iterate[tile_rank], 0.0)
     returned = lax.all_to_all(in_slots, "blk", split_axis=0, concat_axis=0, tiled=True)

time: 321 us -> 233 us (0.73)
  waiting for transfers between devices: 163 us -> 80 us
  blocking collectives: 10.5 us -> 0 us
  starting transfers between devices: 22.7 us -> 32.2 us
  other arithmetic: 82.2 us -> 77.9 us
    psum x3 -> x1, waiting for transfers between devices: 123 us -> 38.6 us  [on_device(): sum_diag, sum_rhs = lax.psum((send_diag, send_rhs), 'src')]
    ppermute x0 -> x6, waiting for transfers between devices: none -> 14.8 us  [on_device(): lax.ppermute(summed, 'src', [(dev, dev ^ hop) for dev in range(4)])]
    all_to_all x1, waiting for transfers between devices: 13.3 us -> 0.01 us  [on_device(): lax.all_to_all(part_vals, 'blk', split_axis=0, concat_axis=0, tiled=True)]
    all_to_all x1 -> x0, blocking collectives: 10.5 us -> none  [on_device(): lax.all_to_all(sum_rhs, 'blk', split_axis=0, concat_axis=0, tiled=True)]
    ppermute x0 -> x6, starting transfers between devices: none -> 4.63 us  [on_device(): lax.ppermute(summed, 'src', [(dev, dev ^ hop) for dev in range(4)])]
    all_to_all x0 -> x1, starting transfers between devices: none -> 4.61 us  [on_device(): lax.all_to_all(sum_rhs, 'blk', split_axis=0, concat_axis=0, tiled=True)]
  transfers between devices with their start and end apart: 9 -> 14, of which waited for: 9 -> 10; matrix products, arithmetic and copies ran while one was open for 4% -> 35% of each run, Pallas kernels for 0% -> 0%
where the time goes in v1:
time: 233 us; the launch traced here: 232 us
  waiting for transfers between devices  80 us (34%)
  other arithmetic  77.9 us (33%)
  starting transfers between devices  32.2 us (14%)
  local copies, waits for them, and re-layouts  27 us (12%)
  between operations  15 us (6%)
    reduce_sum x8, other arithmetic, build(): return jnp.sum(picked, axis=1)  45.3 us
    psum x1, waiting for transfers between devices, on_device(): sum_diag, sum_rhs = lax.psum((send_diag, send_rhs), 'src')  38.6 us
    reduce_sum x3, other arithmetic, on_device(): partial_sum = jnp.sum(dense * nearby[:, None, :], axis=2)  24 us
    ppermute x6, waiting for transfers between devices, on_device(): lax.ppermute(summed, 'src', [(dev, dev ^ hop) for dev in range(4)])  14.8 us
    dynamic_update_slice x8, local copies, waits for them, and re-layouts, tile_matrix(): dense = lax.map(build, (grouped_vals, grouped_lanes))  12.3 us
    all_to_all x1, waiting for transfers between devices, on_device(): lax.all_to_all(part_cols, 'blk', split_axis=0, concat_axis=0, tiled=True)  9.08 us
    all_to_all x1, starting transfers between devices, on_device(): lax.all_to_all(send_keys, 'blk', split_axis=0, concat_axis=0, tiled=True)  6.35 us
    all_to_all x1, waiting for transfers between devices, on_device(): lax.all_to_all(in_slots, 'blk', split_axis=0, concat_axis=0, tiled=True)  5.81 us
  transfers between devices with their start and end apart: 14, of which 10 were waited for; matrix products, arithmetic and copies ran while one was open for 35% of the time, Pallas kernels for 0%

profile of v1, /device:TPU:0, one launch (start us, length us, event | category | flops | bytes accessed | tf_op | source)
XLA Modules:
  0.0 232.2 jit_solution(3877018458897550807)
XLA Ops:
  6.6 0.9 convert_reduce_fusion.1
  7.5 0.7 multiply_add_fusion
  8.4 0.8 gather_fusion.5
  9.2 1.6 broadcast_select_fusion
  10.8 1.6 gather_fusion
  12.4 0.7 select_n.147
  13.1 6.4 %all-to-all-start = ((s32[8,16,1]{1,2,0:T(1,128)}), s32[8,16,1]{1,2,0:T(1,128)S(1)}, u32[]{:S(2)}, u32[]{:S(2)}) async-start(s32[8,16,1]{1,2,0:T(1,128)} %bitcast.3), calls=%async_computation | async-start | bytes 8192 | tf_op jit(solution)/shard_map/all_to_all | solution.py:62
  19.4 2.2 gather_fusion.3
  21.6 0.9 constant_dynamic-slice_fusion
  22.5 2.4 %all-to-all-done = s32[8,16,1]{1,2,0:T(1,128)S(1)} async-done(((s32[8,16,1]{1,2,0:T(1,128)}), s32[8,16,1]{1,2,0:T(1,128)S(1)}, u32[]{:S(2)}, u32[]{:S(2)}) %all-to-all-start) | async-done | bytes 544 | tf_op jit(solution)/shard_map/all_to_all | solution.py:62
  24.9 3.5 %all-to-all-start.2 = ((s32[128,8,128]{2,1,0:T(8,128)}), s32[128,8,128]{2,1,0:T(8,128)S(1)}, u32[]{:S(2)}, u32[]{:S(2)}) async-start(s32[128,8,128]{2,1,0:T(8,128)} %constant_dynamic-slice_fusion), calls=%async_computation.2 | async-start | bytes 1048576 | tf_op jit(solution)/shard_map/all_to_all | solution.py:61
  28.5 0.6 gather_fusion.1
  29.2 0.6 gather_fusion.8
  29.8 0.7 broadcast_select_fusion.4
  31.1 0.7 reduce.7
  31.9 0.6 convert_reduce_fusion.2
  33.9 0.6 gather_fusion.7
  34.6 9.1 %all-to-all-done.2 = s32[128,8,128]{2,1,0:T(8,128)S(1)} async-done(((s32[128,8,128]{2,1,0:T(8,128)}), s32[128,8,128]{2,1,0:T(8,128)S(1)}, u32[]{:S(2)}, u32[]{:S(2)}) %all-to-all-start.2) | async-done | bytes 524320 | tf_op jit(solution)/shard_map/all_to_all | solution.py:61
  43.7 5.2 %reduce-scatter.2.cloned.1.call-done = f32[128,8,128]{2,1,0:T(8,128)} async-done(((f32[128,32,128]{2,1,0:T(8,128)}), f32[128,8,128]{2,1,0:T(8,128)}) %reduce-scatter.2.cloned.1.call-update) | async-done | bytes 524304 | tf_op jit(solution)/shard_map/reduce_scatter | solution.py:52
  48.9 4.6 %all-to-all-start.3 = ((f32[128,8,128]{2,1,0:T(8,128)}), f32[128,8,128]{2,1,0:T(8,128)S(1)}, u32[]{:S(2)}, u32[]{:S(2)}) async-start(f32[128,8,128]{2,1,0:T(8,128)} %reduce-scatter.2.cloned.1.call-done), calls=%async_computation.4 | async-start | bytes 1048576 | tf_op jit(solution)/shard_map/all_to_all | solution.py:56
  53.5 0.7 add_compare_fusion
  54.5 0.8 gather_fusion.4
  55.4 38.6 %all-reduce.4.cloned.1.call-done = (f32[8,16,128]{2,1,0:T(8,128)}, f32[8,16,128]{2,1,0:T(8,128)}) async-done(((f32[8,16,128]{2,1,0:T(8,128)}, f32[8,16,128]{2,1,0:T(8,128)}), (f32[8,16,128]{2,1,0:T(8,128)}, f32[8,16,128]{2,1,0:T(8,128)})) %all-reduce.4.cloned.1.call-update) | async-done | bytes 131088 | tf_op jit(solution)/shard_map/psum | solution.py:53
  94.0 4.6 %all-to-all-start.1 = ((f32[8,16,128]{2,1,0:T(8,128)}), f32[8,16,128]{2,1,0:T(8,128)S(1)}, u32[]{:S(2)}, u32[]{:S(2)}) async-start(f32[8,16,128]{2,1,0:T(8,128)} %get-tuple-element.52), calls=%async_computation.1 | async-start | bytes 131072 | tf_op jit(solution)/shard_map/all_to_all | solution.py:58
  98.6 0.8 gather_fusion.6
  99.6 57.8 %while.11 = (s32[]{:T(128)}, f32[8,16,128,256]{3,2,1,0:T(8,128)}, s32[8,16,8,128]{3,2,1,0:T(8,128)S(1)}, f32[8,16,8,128]{3,2,1,0:T(8,128)S(1)}, s32[]{:T(128)}) while((s32[]{:T(128)}, f32[8,16,128,256]{3,2,1,0:T(8,128)}, s32[8,16,8,128]{3,2,1,0:T(8,128)S(1)}, f32[8,16,8,128]{3,2,1,0:T(8,128)S(1)}, s32[]{:T(128)}) %tuple.23), condition=%wide.region_10.11_spmd.clone, body=%wide.region_8.10_spmd.clone.sunk | while | flops 12058626 | bytes 6685253 | solution.py:23
  99.7 5.7 %select_reduce_fusion.4 = f32[16,128,256]{2,1,0:T(8,128)S(1)} fusion(f32[16,8,128]{2,1,0:T(8,128)S(1)} %dynamic-slice_bitcast_fusion.4, s32[16,8,128]{2,1,0:T(8,128)S(1)} %dynamic-slice_bitcast_fusion.5), kind=kLoop, calls=%fused_computation.16.clone.1 | loop fusion | flops 12058624 | bytes 2228224 | tf_op jit(solution)/shard_map/while/body/eval_jaxpr/reduce_sum | solution.py:21
  105.3 1.6 bitcast_dynamic-update-slice_fusion.2
  106.9 5.7 %select_reduce_fusion.4 = f32[16,128,256]{2,1,0:T(8,128)S(1)} fusion(f32[16,8,128]{2,1,0:T(8,128)S(1)} %dynamic-slice_bitcast_fusion.4, s32[16,8,128]{2,1,0:T(8,128)S(1)} %dynamic-slice_bitcast_fusion.5), kind=kLoop, calls=%fused_computation.16.clone.1 | loop fusion | flops 12058624 | bytes 2228224 | tf_op jit(solution)/shard_map/while/body/eval_jaxpr/reduce_sum | solution.py:21
  112.6 1.5 bitcast_dynamic-update-slice_fusion.2
  114.1 5.7 %select_reduce_fusion.4 = f32[16,128,256]{2,1,0:T(8,128)S(1)} fusion(f32[16,8,128]{2,1,0:T(8,128)S(1)} %dynamic-slice_bitcast_fusion.4, s32[16,8,128]{2,1,0:T(8,128)S(1)} %dynamic-slice_bitcast_fusion.5), kind=kLoop, calls=%fused_computation.16.clone.1 | loop fusion | flops 12058624 | bytes 2228224 | tf_op jit(solution)/shard_map/while/body/eval_jaxpr/reduce_sum | solution.py:21
  119.8 1.5 bitcast_dynamic-update-slice_fusion.2
  121.3 5.7 %select_reduce_fusion.4 = f32[16,128,256]{2,1,0:T(8,128)S(1)} fusion(f32[16,8,128]{2,1,0:T(8,128)S(1)} %dynamic-slice_bitcast_fusion.4, s32[16,8,128]{2,1,0:T(8,128)S(1)} %dynamic-slice_bitcast_fusion.5), kind=kLoop, calls=%fused_computation.16.clone.1 | loop fusion | flops 12058624 | bytes 2228224 | tf_op jit(solution)/shard_map/while/body/eval_jaxpr/reduce_sum | solution.py:21
  127.0 1.5 bitcast_dynamic-update-slice_fusion.2
  128.5 5.7 %select_reduce_fusion.4 = f32[16,128,256]{2,1,0:T(8,128)S(1)} fusion(f32[16,8,128]{2,1,0:T(8,128)S(1)} %dynamic-slice_bitcast_fusion.4, s32[16,8,128]{2,1,0:T(8,128)S(1)} %dynamic-slice_bitcast_fusion.5), kind=kLoop, calls=%fused_computation.16.clone.1 | loop fusion | flops 12058624 | bytes 2228224 | tf_op jit(solution)/shard_map/while/body/eval_jaxpr/reduce_sum | solution.py:21
  134.2 1.6 bitcast_dynamic-update-slice_fusion.2
  135.8 5.7 %select_reduce_fusion.4 = f32[16,128,256]{2,1,0:T(8,128)S(1)} fusion(f32[16,8,128]{2,1,0:T(8,128)S(1)} %dynamic-slice_bitcast_fusion.4, s32[16,8,128]{2,1,0:T(8,128)S(1)} %dynamic-slice_bitcast_fusion.5), kind=kLoop, calls=%fused_computation.16.clone.1 | loop fusion | flops 12058624 | bytes 2228224 | tf_op jit(solution)/shard_map/while/body/eval_jaxpr/reduce_sum | solution.py:21
  141.5 1.5 bitcast_dynamic-update-slice_fusion.2
  143.0 5.7 %select_reduce_fusion.4 = f32[16,128,256]{2,1,0:T(8,128)S(1)} fusion(f32[16,8,128]{2,1,0:T(8,128)S(1)} %dynamic-slice_bitcast_fusion.4, s32[16,8,128]{2,1,0:T(8,128)S(1)} %dynamic-slice_bitcast_fusion.5), kind=kLoop, calls=%fused_computation.16.clone.1 | loop fusion | flops 12058624 | bytes 2228224 | tf_op jit(solution)/shard_map/while/body/eval_jaxpr/reduce_sum | solution.py:21
  148.7 1.6 bitcast_dynamic-update-slice_fusion.2
  150.2 5.7 %select_reduce_fusion.4 = f32[16,128,256]{2,1,0:T(8,128)S(1)} fusion(f32[16,8,128]{2,1,0:T(8,128)S(1)} %dynamic-slice_bitcast_fusion.4, s32[16,8,128]{2,1,0:T(8,128)S(1)} %dynamic-slice_bitcast_fusion.5), kind=kLoop, calls=%fused_computation.16.clone.1 | loop fusion | flops 12058624 | bytes 2228224 | tf_op jit(solution)/shard_map/while/body/eval_jaxpr/reduce_sum | solution.py:21
  155.9 1.5 bitcast_dynamic-update-slice_fusion.2
  157.4 8.0 %multiply_reduce_fusion.2 = f32[8,16,128]{2,1,0:T(8,128)S(1)} fusion(f32[8,16,128,256]{3,2,1,0:T(8,128)} %get-tuple-element.32, f32[8,16,256]{2,1,0:T(8,128)S(1)} %bitcast.66), kind=kLoop, calls=%fused_computation.22 | loop fusion | flops 8372224 | bytes 16973824 | tf_op jit(solution)/shard_map/reduce_sum | solution.py:80
  165.4 1.5 collective-permute-start
  167.0 5.1 %all-to-all-start.4 = ((f32[8,16,128]{2,1,0:T(8,128)}), f32[8,16,128]{2,1,0:T(8,128)S(1)}, u32[]{:S(2)}, u32[]{:S(2)}) async-start(f32[8,16,128]{2,1,0:T(8,128)} %get-tuple-element.51), calls=%async_computation.5 | async-start | bytes 131072 | tf_op jit(solution)/shard_map/all_to_all | solution.py:57
  172.7 0.6 iota_compare_fusion.4
  173.4 0.6 gather_fusion.2
  174.0 4.0 %all-to-all-done.4 = f32[8,16,128]{2,1,0:T(8,128)S(1)} async-done(((f32[8,16,128]{2,1,0:T(8,128)}), f32[8,16,128]{2,1,0:T(8,128)S(1)}, u32[]{:S(2)}, u32[]{:S(2)}) %all-to-all-start.4) | async-done | bytes 65568 | tf_op jit(solution)/shard_map/all_to_all | solution.py:57
  178.0 0.6 gather_fusion.9
  178.7 0.6 gather_fusion.10
  179.4 8.0 %multiply_reduce_fusion.1 = f32[8,16,128]{2,1,0:T(8,128)S(1)} fusion(f32[8,16,128,256]{3,2,1,0:T(8,128)} %get-tuple-element.32, f32[8,16,256]{2,1,0:T(8,128)S(1)} %bitcast.68), kind=kLoop, calls=%fused_computation.21 | loop fusion | flops 8372224 | bytes 16973824 | tf_op jit(solution)/shard_map/reduce_sum | solution.py:80
  187.4 0.6 collective-permute-start.2
  188.1 3.7 %collective-permute-done.2 = f32[128,128]{1,0:T(8,128)S(1)} collective-permute-done((f32[128,128]{1,0:T(8,128)S(1)}, f32[128,128]{1,0:T(8,128)S(1)}, u32[]{:S(2)}, u32[]{:S(2)}) %collective-permute-start.2) | collective-permute-done | bytes 65568 | tf_op jit(solution)/shard_map/ppermute | solution.py:83
  192.4 3.7 %collective-permute-done.3 = f32[128,128]{1,0:T(8,128)S(1)} collective-permute-done((f32[128,128]{1,0:T(8,128)S(1)}, f32[128,128]{1,0:T(8,128)S(1)}, u32[]{:S(2)}, u32[]{:S(2)}) %collective-permute-start.3) | collective-permute-done | bytes 65568 | tf_op jit(solution)/shard_map/ppermute | solution.py:83
  196.2 0.6 gather_fusion.11
  196.9 8.0 %multiply_reduce_fusion = f32[8,16,128]{2,1,0:T(8,128)S(1)} fusion(f32[8,16,128,256]{3,2,1,0:T(8,128)} %get-tuple-element.32, f32[8,16,256]{2,1,0:T(8,128)S(1)} %bitcast.67), kind=kLoop, calls=%fused_computation.20 | loop fusion | flops 8372224 | bytes 16973824 | tf_op jit(solution)/shard_map/reduce_sum | solution.py:80
  204.9 0.6 collective-permute-start.4
  205.5 3.7 %collective-permute-done.4 = f32[128,128]{1,0:T(8,128)S(1)} collective-permute-done((f32[128,128]{1,0:T(8,128)S(1)}, f32[128,128]{1,0:T(8,128)S(1)}, u32[]{:S(2)}, u32[]{:S(2)}) %collective-permute-start.4) | collective-permute-done | bytes 65568 | tf_op jit(solution)/shard_map/ppermute | solution.py:83
  209.8 3.7 %collective-permute-done.5 = f32[128,128]{1,0:T(8,128)S(1)} collective-permute-done((f32[128,128]{1,0:T(8,128)S(1)}, f32[128,128]{1,0:T(8,128)S(1)}, u32[]{:S(2)}, u32[]{:S(2)}) %collective-permute-start.5) | collective-permute-done | bytes 65568 | tf_op jit(solution)/shard_map/ppermute | solution.py:83
  213.6 0.6 gather_fusion.12
  214.3 0.7 broadcast_select_fusion.2
  215.0 3.3 %all-to-all-start.5 = ((f32[8,16,128]{2,1,0:T(8,128)}), f32[8,16,128]{2,1,0:T(8,128)S(1)}, u32[]{:S(2)}, u32[]{:S(2)}) async-start(f32[8,16,128]{2,1,0:T(8,128)} %broadcast_select_fusion.2), calls=%async_computation.6 | async-start | bytes 131072 | tf_op jit(solution)/shard_map/all_to_all | solution.py:86
  218.4 5.8 %all-to-all-done.5 = f32[8,16,128]{2,1,0:T(8,128)S(1)} async-done(((f32[8,16,128]{2,1,0:T(8,128)}), f32[8,16,128]{2,1,0:T(8,128)S(1)}, u32[]{:S(2)}, u32[]{:S(2)}) %all-to-all-start.5) | async-done | bytes 65568 | tf_op jit(solution)/shard_map/all_to_all | solution.py:86
  224.2 1.2 gather_fusion.13
  (69 shorter events, 4.1 us)
Async XLA Ops:
  6.5 1.9 copy-start
  6.5 22.0 %copy-start.2 = (f32[1,64,128]{2,1,0:T(8,128)S(1)}, f32[1,64,128]{2,1,0:T(8,128)}, u32[]{:S(2)}) copy-start(f32[1,64,128]{2,1,0:T(8,128)} %param.11) | copy-start | bytes 98308
  6.5 22.0 %copy-start.3 = (s32[64,128]{1,0:T(8,128)S(1)}, s32[64,128]{1,0:T(8,128)}, u32[]{:S(2)}) copy-start(s32[64,128]{1,0:T(8,128)} %param.12) | copy-start | bytes 98308
  6.5 22.6 %copy-start.1 = (f32[1,64,128]{2,1,0:T(8,128)S(1)}, f32[1,64,128]{2,1,0:T(8,128)}, u32[]{:S(2)}) copy-start(f32[1,64,128]{2,1,0:T(8,128)} %param.10) | copy-start | bytes 98308
  6.5 42.3 %reduce-scatter.2.cloned.1.call-start = ((), (), s32[]{:S(2)}) async-start(), calls=%async_computation.7 | async-start | bytes 2621440 | tf_op jit(solution)/shard_map/reduce_scatter | solution.py:52
  13.1 11.9 %all-to-all-start = ((s32[8,16,1]{1,2,0:T(1,128)}), s32[8,16,1]{1,2,0:T(1,128)S(1)}, u32[]{:S(2)}, u32[]{:S(2)}) async-start(s32[8,16,1]{1,2,0:T(1,128)} %bitcast.3), calls=%async_computation | async-start | bytes 8192 | tf_op jit(solution)/shard_map/all_to_all | solution.py:62
  24.9 18.8 %all-to-all-start.2 = ((s32[128,8,128]{2,1,0:T(8,128)}), s32[128,8,128]{2,1,0:T(8,128)S(1)}, u32[]{:S(2)}, u32[]{:S(2)}) async-start(s32[128,8,128]{2,1,0:T(8,128)} %constant_dynamic-slice_fusion), calls=%async_computation.2 | async-start | bytes 1048576 | tf_op jit(solution)/shard_map/all_to_all | solution.py:61
  28.4 65.6 %all-reduce.4.cloned.1.call-start = ((), (), s32[]{:S(2)}) async-start(), calls=%async_computation.8 | async-start | bytes 262144 | tf_op jit(solution)/shard_map/psum | solution.py:53
  48.9 45.2 %all-to-all-start.3 = ((f32[128,8,128]{2,1,0:T(8,128)}), f32[128,8,128]{2,1,0:T(8,128)S(1)}, u32[]{:S(2)}, u32[]{:S(2)}) async-start(f32[128,8,128]{2,1,0:T(8,128)} %reduce-scatter.2.cloned.1.call-done), calls=%async_computation.4 | async-start | bytes 1048576 | tf_op jit(solution)/shard_map/all_to_all | solution.py:56
  94.0 72.9 %all-to-all-start.1 = ((f32[8,16,128]{2,1,0:T(8,128)}), f32[8,16,128]{2,1,0:T(8,128)S(1)}, u32[]{:S(2)}, u32[]{:S(2)}) async-start(f32[8,16,128]{2,1,0:T(8,128)} %get-tuple-element.52), calls=%async_computation.1 | async-start | bytes 131072 | tf_op jit(solution)/shard_map/all_to_all | solution.py:58
  165.4 6.6 %collective-permute-start = (f32[128,128]{1,0:T(8,128)S(1)}, f32[128,128]{1,0:T(8,128)S(1)}, u32[]{:S(2)}, u32[]{:S(2)}) collective-permute-start(f32[128,128]{1,0:T(8,128)S(1)} %bitcast.69), channel_id=1, source_target_pairs={{0,8},{8,0},{16,24},{24,16},{1,9},{9,1},{17,25},{25,17},{2,10},{10... | collective-permute-start | bytes 196616 | tf_op jit(solution)/shard_map/ppermute | solution.py:83
  167.0 11.0 %all-to-all-start.4 = ((f32[8,16,128]{2,1,0:T(8,128)}), f32[8,16,128]{2,1,0:T(8,128)S(1)}, u32[]{:S(2)}, u32[]{:S(2)}) async-start(f32[8,16,128]{2,1,0:T(8,128)} %get-tuple-element.51), calls=%async_computation.5 | async-start | bytes 131072 | tf_op jit(solution)/shard_map/all_to_all | solution.py:57
  172.1 6.5 %collective-permute-start.1 = (f32[128,128]{1,0:T(8,128)S(1)}, f32[128,128]{1,0:T(8,128)S(1)}, u32[]{:S(2)}, u32[]{:S(2)}) collective-permute-start(f32[128,128]{1,0:T(8,128)S(1)} %bitcast_add_fusion.3), channel_id=1, source_target_pairs={{0,16},{8,24},{16,0},{24,8},{1,17},{9,25},{17,1},{25,9},{2,18},{10... | collective-permute-start | bytes 196616 | tf_op jit(solution)/shard_map/ppermute | solution.py:83
  179.4 39.0 %copy-start.4 = (s32[64,1]{0,1:T(1,128)S(1)}, s32[64,1]{0,1:T(1,128)}, u32[]{:S(2)}) copy-start(s32[64,1]{0,1:T(1,128)} %param.14) | copy-start | bytes 772
  187.4 4.3 %collective-permute-start.2 = (f32[128,128]{1,0:T(8,128)S(1)}, f32[128,128]{1,0:T(8,128)S(1)}, u32[]{:S(2)}, u32[]{:S(2)}) collective-permute-start(f32[128,128]{1,0:T(8,128)S(1)} %bitcast.71), channel_id=1, source_target_pairs={{0,8},{8,0},{16,24},{24,16},{1,9},{9,1},{17,25},{25,17},{2,10},{10... | collective-permute-start | bytes 196616 | tf_op jit(solution)/shard_map/ppermute | solution.py:83
  191.8 4.3 %collective-permute-start.3 = (f32[128,128]{1,0:T(8,128)S(1)}, f32[128,128]{1,0:T(8,128)S(1)}, u32[]{:S(2)}, u32[]{:S(2)}) collective-permute-start(f32[128,128]{1,0:T(8,128)S(1)} %bitcast_add_fusion.2), channel_id=1, source_target_pairs={{0,16},{8,24},{16,0},{24,8},{1,17},{9,25},{17,1},{25,9},{2,18},{10... | collective-permute-start | bytes 196616 | tf_op jit(solution)/shard_map/ppermute | solution.py:83
  204.9 4.3 %collective-permute-start.4 = (f32[128,128]{1,0:T(8,128)S(1)}, f32[128,128]{1,0:T(8,128)S(1)}, u32[]{:S(2)}, u32[]{:S(2)}) collective-permute-start(f32[128,128]{1,0:T(8,128)S(1)} %bitcast.70), channel_id=1, source_target_pairs={{0,8},{8,0},{16,24},{24,16},{1,9},{9,1},{17,25},{25,17},{2,10},{10... | collective-permute-start | bytes 196616 | tf_op jit(solution)/shard_map/ppermute | solution.py:83
  209.2 4.3 %collective-permute-start.5 = (f32[128,128]{1,0:T(8,128)S(1)}, f32[128,128]{1,0:T(8,128)S(1)}, u32[]{:S(2)}, u32[]{:S(2)}) collective-permute-start(f32[128,128]{1,0:T(8,128)S(1)} %bitcast_add_fusion.1), channel_id=1, source_target_pairs={{0,16},{8,24},{16,0},{24,8},{1,17},{9,25},{17,1},{25,9},{2,18},{10... | collective-permute-start | bytes 196616 | tf_op jit(solution)/shard_map/ppermute | solution.py:83
  215.0 9.2 %all-to-all-start.5 = ((f32[8,16,128]{2,1,0:T(8,128)}), f32[8,16,128]{2,1,0:T(8,128)S(1)}, u32[]{:S(2)}, u32[]{:S(2)}) async-start(f32[8,16,128]{2,1,0:T(8,128)} %broadcast_select_fusion.2), calls=%async_computation.6 | async-start | bytes 131072 | tf_op jit(solution)/shard_map/all_to_all | solution.py:86
Sparse Core Ops, SparseCore 0:
  10.9 37.9 reduce-scatter.1
  51.7 42.2 all-reduce.3
